TPU v7x, 32 devices: a whole 2x2x4 slice. The times are simulated.
32 devices in a mesh: seq: 8 (over y, x, core), dp: 4 (over z).
Axes of the slice: x: 2, y: 2, z: 4, core: 2. Of those that a mesh axis runs over, the one named last changes fastest.
Arguments:
- queries: bfloat16 [4, 3072, 2048], P('dp', 'seq'), may hold values from -40 to 40
- keys: bfloat16 [4, 3072, 2048], P('dp', 'seq'), may hold values from -40 to 40
- values: bfloat16 [4, 3072, 2048], P('dp', 'seq'), may hold values from -6 to 6
- out_grad: bfloat16 [4, 3072, 2048], P('dp', 'seq'), may hold values from -6 to 6
- proj_weight: bfloat16 [2048, 2048], P('dp'), may hold values from -0.125 to 0.125
- lengths: int32 [4], P('dp'), may hold values from 768 to 3072
Outputs:
- query_grad: bfloat16 [4, 3072, 2048], P('dp', 'seq')
- key_grad: bfloat16 [4, 3072, 2048], P('dp', 'seq')
- value_grad: bfloat16 [4, 3072, 2048], P('dp', 'seq')
- weight_grad: float32 [2048, 2048], P('dp', 'seq')
All inputs are finite; a program needn't handle non-finite values.
Results may differ from a plain program's by a relative error of at most 0.019.
Values may be sent and summed in bfloat16 or wider, within the bound.
A program may use at most 192 MiB of HBM per device.

v0:
```python
import functools

import jax
import jax.numpy as jnp
from jax import lax
from jax.experimental import pallas as pl
from jax.experimental.pallas import tpu as pltpu
from jax.sharding import PartitionSpec as P

HEAD_DIM = 128
PAIR = 2 * HEAD_DIM
LOG2E = 1.4426950408889634
NEG = -1e30
MESH = pl.DeviceIdType.MESH

NT = (((1,), (1,)), ((), ()))
NN = (((1,), (0,)), ((), ()))
TN = (((0,), (0,)), ((), ()))


def dot(a, b, dims):
    return lax.dot_general(a, b, dims, preferred_element_type=jnp.float32)


def flip(i, bit):
    return i + bit - 2 * bit * lax.rem(i // bit, 2)


def shard_order(count):
    return [sorted(range(count), key=lambda d: (abs(d - z), d < z)) for z in range(count)]


def pick(table, z, s):
    found = jnp.int32(0)
    for zz, row in enumerate(table):
        for ss, value in enumerate(row):
            found = found + jnp.where(z == zz, jnp.where(s == ss, value, 0), 0)
    return found


def every(count, body):
    def step(index, carry):
        body(index)
        return carry

    lax.fori_loop(0, count, step, 0)


def kernel(n, nd, len_ref, q_hbm, k_hbm, v_hbm, g_hbm, w_hbm, dq_hbm, dk_hbm, dv_hbm, wg_hbm, *scratch):
    (
        q_buf, kv, far, near, t0, t1in, behind, relay, do_buf, dq_buf, o_buf, o_in,
        g_buf, g_mine, g_send, g_in, w_buf, y_send, y_in, z_buf, z_in, kept, acc, x_send, x_in, out_buf,
        q_l, kv_l, g_l, w_l, dq_s, out_s,
        far_s, far_r, near_s, near_r, t1_s, t1_r, ret_s, ret_r, rel_s, rel_r,
        o_s, o_r, g_s, g_r, wu_s, wd_s, w_r, wp_s, wp_r, y_s, y_r, z_s, z_r, x_s, x_r,
    ) = scratch
    f32, bf16 = jnp.float32, jnp.bfloat16
    i, z = lax.axis_index("seq"), lax.axis_index("dp")
    steps, _, _, tokens, _ = kv.shape
    per = steps // nd
    chips = n // 2
    chip = i // 2
    par = lax.rem(i, 2)
    mate = flip(i, 1)
    ahead, back = lax.rem(i + 2, n), lax.rem(i + n - 2, n)
    across = flip(i, n // 2)
    beside = flip(i, 2)
    relayed = n == 8
    width = w_hbm.shape[1]
    half = width // 2
    own = width // n
    span = half // 2
    table = shard_order(nd)

    def pair_at(it):
        return pick(table, z, it // per) * per + lax.rem(it, per)

    def rdma(src, dst, send, recv, **where):
        return pltpu.make_async_remote_copy(
            src_ref=src, dst_ref=dst, send_sem=send, recv_sem=recv, device_id=where, device_id_type=MESH
        )

    def columns(start, size):
        return pl.ds(pl.multiple_of(start, 128), size)

    def load_kv(it):
        at = pair_at(it) * PAIR
        for a in range(2):
            for b, ref in enumerate((k_hbm, v_hbm)):
                src = ref.at[:, columns(at + a * HEAD_DIM, HEAD_DIM)]
                pltpu.make_async_copy(src, kv.at[it, a, b], kv_l.at[it]).start()

    def load_q(it):
        at = pair_at(it) * PAIR
        for a in range(2):
            src = q_hbm.at[:, columns(at + a * HEAD_DIM, HEAD_DIM)]
            pltpu.make_async_copy(src, q_buf.at[it, a], q_l.at[it]).start()

    every(steps, load_kv)
    load_g = pltpu.make_async_copy(g_hbm, g_buf, g_l.at[0])
    load_g.start()
    own_w = []
    for k in range(per):
        for h in range(2):
            src = w_hbm.at[pl.ds(k * PAIR, PAIR), pl.ds(h * half, half)]
            own_w.append(pltpu.make_async_copy(src, w_buf.at[z * per + k, h], w_l.at[2 * k + h]))
            own_w[-1].start()
    every(steps, load_q)

    bits = []
    bit = n // 2
    while bit > 1:
        bits.append(bit)
        bit //= 2
    greet = [dict(seq=mate), dict(seq=ahead), dict(seq=back)]
    greet += [dict(seq=flip(i, b)) for b in bits]
    greet += [dict(dp=lax.rem(z + s, nd)) for s in range(1, nd)]
    barrier = pltpu.get_barrier_semaphore()
    for who in greet:
        pl.semaphore_signal(barrier, inc=1, device_id=who, device_id_type=MESH)

    @pl.when(chip == 0)
    def _():
        def clear(it):
            far[it] = jnp.zeros_like(far[it])

        every(steps, clear)

    pl.semaphore_wait(barrier, len(greet))

    def far_copy(it, a):
        return rdma(kv.at[it, a], far.at[it, a], far_s.at[2 * it + a], far_r.at[2 * it + a], seq=ahead)

    def far_relay_in(it):
        return rdma(kv.at[it, 1], relay.at[it], far_s.at[2 * it + 1], rel_r.at[it], seq=across)

    def far_relay_out(it):
        return rdma(relay.at[it], far.at[it, 1], rel_s.at[it], far_r.at[2 * it + 1], seq=beside)

    def ret_copy(it, a):
        return rdma(far.at[it, a], behind.at[it, a], ret_s.at[2 * it + a], ret_r.at[2 * it + a], seq=back)

    def ret_relay_in(it):
        return rdma(far.at[it, 1], relay.at[it], ret_s.at[2 * it + 1], rel_r.at[it], seq=across)

    def ret_relay_out(it):
        return rdma(relay.at[it], behind.at[it, 1], rel_s.at[it], ret_r.at[2 * it + 1], seq=beside)

    def near_copy(src, it, a):
        return rdma(src.at[it, a], near.at[it, a], near_s.at[2 * it + a], near_r.at[2 * it + a], seq=mate)

    def t1_copy(it, a):
        return rdma(near.at[it, a], t1in.at[it, a], t1_s.at[2 * it + a], t1_r.at[2 * it + a], seq=mate)

    def o_copy(it):
        return rdma(o_buf.at[it], o_in.at[it], o_s.at[it], o_r.at[it], seq=mate)

    def w_up(piece):
        return rdma(w_buf.at[piece, par], w_buf.at[piece, par], wu_s.at[piece], w_r.at[piece], dp=lax.rem(z + 1, nd))

    def w_down(piece):
        return rdma(w_buf.at[piece, par], w_buf.at[piece, par], wd_s.at[piece], w_r.at[piece], dp=lax.rem(z + nd - 1, nd))

    def w_mate(piece, side):
        return rdma(w_buf.at[piece, side], w_buf.at[piece, side], wp_s.at[piece], wp_r.at[piece], seq=mate)

    def y_copy(it):
        return rdma(y_send.at[it], y_in.at[it], y_s.at[it], y_r.at[it], seq=across)

    def z_copy(it, source, shard):
        k = lax.rem(it, per)
        return rdma(z_buf.at[it], z_in.at[source, k], z_s.at[it], z_r.at[source * per + k], dp=shard)

    def first_sends(it):
        pltpu.make_async_copy(kv.at[it], kv.at[it], kv_l.at[it]).wait()

        @pl.when(chip < chips - 1)
        def _():
            far_copy(it, 0).start()
            if relayed:
                pl.when(chip != 1)(lambda: far_copy(it, 1).start())
                pl.when(chip == 1)(lambda: far_relay_in(it).start())
            else:
                far_copy(it, 1).start()

        @pl.when(par == 0)
        def _():
            for a in range(2):
                near_copy(kv, it, a).start()

    every(steps, first_sends)

    for copy in own_w:
        copy.wait()
    for k in range(per):
        pl.when(z < nd - 1)(lambda: w_up(z * per + k).start())
        pl.when(z > 0)(lambda: w_down(z * per + k).start())

    load_g.wait()
    at_row = i * tokens + lax.broadcasted_iota(jnp.int32, (tokens, 1), 0)
    live = at_row < len_ref[0]
    for c in range(chips):
        first = g_buf[:, 2 * c * own : (2 * c + 1) * own].astype(f32)
        second = g_buf[:, (2 * c + 1) * own : (2 * c + 2) * own].astype(f32)
        first, second = jnp.where(live, first, 0.0), jnp.where(live, second, 0.0)
        g_buf[:, 2 * c * own : (2 * c + 2) * own] = jnp.concatenate([first, second], 1).astype(bf16)
        g_mine[c * own : (c + 1) * own, :] = jnp.where(par == 0, first, second).T.astype(bf16)
        g_send[c * own : (c + 1) * own, :] = jnp.where(par == 0, second, first).T.astype(bf16)
    g_copy = rdma(g_send, g_in, g_s.at[0], g_r.at[0], seq=mate)
    g_copy.start()

    def halo_relay(it):
        far_relay_in(it).wait_recv()
        far_relay_out(it).start()

    if relayed:
        pl.when(chip == chips - 1)(lambda: halo_relay(0))

    g_copy.wait_recv()
    scale = HEAD_DIM ** (-0.5)
    c_exp = scale * LOG2E

    def begin(it):
        @pl.when(chip > 0)
        def _():
            for a in range(2):
                far_copy(it, a).wait_recv()

        @pl.when(par == 1)
        def _():
            for a in range(2):
                near_copy(far, it, a).start()

        if relayed:
            for extra in (1, 2):

                @pl.when(jnp.logical_and(chip == chips - 1, 2 * it + extra < steps))
                def _():
                    halo_relay(2 * it + extra)

        piece = pair_at(it)

        @pl.when(it >= per)
        def _():
            w_mate(piece, 1 - par).wait_recv()

        do = dot(g_buf[:, :half], w_buf[piece, 0], NT) + dot(g_buf[:, half:], w_buf[piece, 1], NT)
        do_buf[...] = do.astype(bf16)

    def attend(it):
        causal_keys = lax.broadcasted_iota(jnp.int32, (tokens, tokens), 0)
        causal_queries = lax.broadcasted_iota(jnp.int32, (tokens, tokens), 1)
        for a in range(2):
            near_copy(kv, it, a).wait_recv()
            q = q_buf[it, a]
            sources = (kv, near, far)
            parts, tops = [], []
            for offset, source in enumerate(sources):
                s = dot(source[it, a, 0], q, NT)
                if offset == 0:
                    s = jnp.where(causal_keys <= causal_queries, s, NEG)
                parts.append(s)
                top = jnp.max(s, axis=0, keepdims=True)
                if offset:
                    top = top + jnp.where(i >= offset, 0.0, NEG)
                tops.append(top)
            top = functools.reduce(jnp.maximum, tops) * c_exp
            total = None
            for offset in range(3):
                shift = top if offset == 0 else top + jnp.where(i >= offset, 0.0, -NEG)
                parts[offset] = jnp.exp2(parts[offset] * c_exp - shift)
                t = jnp.sum(parts[offset], axis=0, keepdims=True)
                total = t if total is None else total + t
            inverse = 1.0 / total
            out = None
            for offset, source in enumerate(sources):
                parts[offset] = parts[offset] * inverse
                o = dot(source[it, a, 1], parts[offset].astype(bf16), TN)
                out = o if out is None else out + o
            o = out.T.astype(bf16)
            o_buf[it, :, a * HEAD_DIM : (a + 1) * HEAD_DIM] = o
            do = do_buf[:, a * HEAD_DIM : (a + 1) * HEAD_DIM]
            delta = jnp.sum((do.astype(f32) * o.astype(f32)).T, axis=0, keepdims=True)
            near_copy(kv, it, a).wait_send()
            dq = None
            for offset, (source, term) in enumerate(zip(sources, (t0, near, far))):
                k, v = source[it, a, 0], source[it, a, 1]
                p = parts[offset]
                dv = dot(p.astype(bf16), do, NN)
                ds = (p * (dot(v, do, NT) - delta)).astype(bf16)
                dk = dot(ds, q, NN) * scale
                part = dot(k, ds, TN)
                dq = part if dq is None else dq + part
                term[it, a, 0] = dk.astype(bf16)
                term[it, a, 1] = dv.astype(bf16)
                if offset == 1:
                    t1_copy(it, a).start()
            dq_buf[it, :, a * HEAD_DIM : (a + 1) * HEAD_DIM] = (dq * scale).T.astype(bf16)
        o_copy(it).start()
        pltpu.make_async_copy(dq_buf.at[it], dq_hbm.at[:, columns(pair_at(it) * PAIR, PAIR)], dq_s.at[it]).start()

    def move_weights(it):
        j = it - 1
        below, above = z - 1 - j // per, z + 1 + j // per

        @pl.when(jnp.logical_and(it >= 1, below >= 0))
        def _():
            piece = below * per + lax.rem(j, per)
            w_up(piece).wait_recv()
            pl.when(z < nd - 1)(lambda: w_up(piece).start())
            w_mate(piece, par).start()

        @pl.when(jnp.logical_and(it >= 1, above <= nd - 1))
        def _():
            piece = above * per + lax.rem(j, per)
            w_down(piece).wait_recv()
            pl.when(z > 0)(lambda: w_down(piece).start())
            w_mate(piece, par).start()

    high = lax.rem(i // bits[0], 2)

    def stage_a(m):
        for a in range(2):
            t1_copy(m, a).wait_recv()

            @pl.when(par == 1)
            def _():
                far[m, a] = (far[m, a].astype(f32) + t1in[m, a].astype(f32)).astype(bf16)

        @pl.when(chip > 0)
        def _():
            ret_copy(m, 0).start()
            if relayed:
                pl.when(chip != 2)(lambda: ret_copy(m, 1).start())
                pl.when(chip == 2)(lambda: ret_relay_in(m).start())
            else:
                ret_copy(m, 1).start()

        o_copy(m).wait_recv()

        def product(side):
            rows = pl.ds(pl.multiple_of(side * span, span), span)
            return dot(g_mine[rows, :], o_buf[m], NN) + dot(g_in[rows, :], o_in[m], NN)

        y_send[m] = product(1 - high).astype(bf16)
        y_copy(m).start()
        kept[lax.rem(m, 2)] = product(high)

    def stage_b(m):
        y_copy(m).wait_recv()
        total = kept[lax.rem(m, 2)] + y_in[m].astype(f32)

        @pl.when(m < per)
        def _():
            acc[lax.rem(m, per)] = total

        @pl.when(m >= per)
        def _():
            z_buf[m] = total.astype(bf16)
            z_copy(m, z, pick(table, z, m // per)).start()

        if relayed:

            @pl.when(chip == 0)
            def _():
                ret_relay_in(m).wait_recv()
                ret_relay_out(m).start()

    def step(it):
        pl.when(it < steps)(lambda: begin(it))
        pl.when(jnp.logical_and(it >= 1, it <= steps))(lambda: stage_a(it - 1))
        pl.when(it >= 2)(lambda: stage_b(it - 2))

        @pl.when(it < steps)
        def _():
            pltpu.make_async_copy(q_buf.at[it], q_buf.at[it], q_l.at[it]).wait()
            attend(it)
            pl.when(it < steps - 1)(lambda: move_weights(it))

    every(steps + 2, step)

    def finish(m):
        @pl.when(chip < chips - 1)
        def _():
            for a in range(2):
                ret_copy(m, a).wait_recv()

        for a in range(2):
            for b, out in enumerate((dk_hbm, dv_hbm)):
                total = t0[m, a, b].astype(f32)
                total = total + jnp.where(par == 0, t1in[m, a, b].astype(f32), 0.0)
                total = total + jnp.where(chip < chips - 1, behind[m, a, b].astype(f32), 0.0)
                t0[m, a, b] = total.astype(bf16)
                dst = out.at[:, columns(pair_at(m) * PAIR + a * HEAD_DIM, HEAD_DIM)]
                pltpu.make_async_copy(t0.at[m, a, b], dst, out_s.at[m]).start()

    every(steps - 1, finish)

    for s in range(1, nd):
        source = lax.rem(z + s, nd)
        for k in range(per):
            z_copy(per + k, source, z).wait_recv()
            acc[k] = acc[k] + z_in[source, k].astype(f32)
    base = jnp.int32(0)
    rows = span
    sent = []
    for level, b in enumerate(bits[1:]):
        rows //= 2
        up = lax.rem(i // b, 2)
        away = pl.ds(pl.multiple_of(base + (1 - up) * rows, rows), rows)
        base = base + up * rows
        stay = pl.ds(pl.multiple_of(base, rows), rows)
        at = pl.ds(span - 2 * rows, rows)
        for k in range(per):
            x_send[k, at, :] = acc[k, away, :].astype(bf16)
            sent.append(
                rdma(
                    x_send.at[k, at, :], x_in.at[k, at, :],
                    x_s.at[level * per + k], x_r.at[level * per + k], seq=flip(i, b),
                )
            )
            sent[-1].start()
        if level == 0:
            finish(steps - 1)
        for k in range(per):
            sent[-per + k].wait_recv()
            acc[k, stay, :] = acc[k, stay, :] + x_in[k, at, :].astype(f32)
    mine = pl.ds(pl.multiple_of(base, own), own)
    for k in range(per):
        out_buf[k * PAIR : (k + 1) * PAIR, :] = acc[k, mine, :].T
    put = pltpu.make_async_copy(out_buf, wg_hbm, g_l.at[0])
    put.start()

    def settle(m):
        for a in range(2):
            pl.when(chip < chips - 1)(lambda: far_copy(m, a).wait_send())
            pl.when(chip > 0)(lambda: ret_copy(m, a).wait_send())
            t1_copy(m, a).wait_send()
        if relayed:
            pl.when(chip == 0)(lambda: ret_relay_out(m).wait_send())
            pl.when(chip == chips - 1)(lambda: far_relay_out(m).wait_send())
        o_copy(m).wait_send()
        y_copy(m).wait_send()

        @pl.when(m >= per)
        def _():
            z_copy(m, z, pick(table, z, m // per)).wait_send()
            w_mate(pair_at(m), par).wait_send()

        pl.when(jnp.logical_and(z < nd - 1, m < (z + 1) * per))(lambda: w_up(m).wait_send())
        pl.when(jnp.logical_and(z > 0, m >= z * per))(lambda: w_down(m).wait_send())
        pltpu.make_async_copy(dq_buf.at[m], dq_hbm.at[:, columns(pair_at(m) * PAIR, PAIR)], dq_s.at[m]).wait()
        pltpu.make_async_copy(t0.at[m], t0.at[m], out_s.at[m]).wait()

    every(steps, settle)
    g_copy.wait_send()
    for copy in sent:
        copy.wait_send()
    put.wait()


def layer(n, nd, queries, keys, values, out_grad, proj_weight, lengths):
    f32, bf16 = jnp.float32, jnp.bfloat16
    tokens, feat = queries.shape[1:]
    rows, width = proj_weight.shape
    steps = feat // PAIR
    per = rows // PAIR
    half = width // 2
    span = half // 2
    own = width // n
    head = (steps, 2, tokens, HEAD_DIM)
    both = (steps, 2, 2, tokens, HEAD_DIM)
    pair = (steps, tokens, PAIR)
    levels = max(1, n.bit_length() - 3)
    vmem = [
        (head, bf16),
        *[(both, bf16)] * 6,
        ((steps, 2, tokens, HEAD_DIM), bf16),
        ((tokens, PAIR), bf16),
        *[(pair, bf16)] * 3,
        ((tokens, width), bf16),
        *[((half, tokens), bf16)] * 3,
        ((steps, 2, PAIR, half), bf16),
        *[((steps, span, PAIR), bf16)] * 3,
        ((nd, per, span, PAIR), bf16),
        ((2, span, PAIR), f32),
        ((per, span, PAIR), f32),
        *[((per, span, PAIR), bf16)] * 2,
        ((rows, own), f32),
    ]
    sems = [steps, steps, 1, 2 * per, steps, steps]
    sems += [2 * steps] * 8 + [steps] * 2
    sems += [steps, steps, 1, 1] + [steps] * 5 + [steps] * 3 + [nd * per] + [levels * per] * 2
    anywhere = pl.BlockSpec(memory_space=pl.ANY)
    grad = jax.ShapeDtypeStruct((tokens, feat), bf16)
    dq, dk, dv, wg = pl.pallas_call(
        functools.partial(kernel, n, nd),
        in_specs=[pl.BlockSpec(memory_space=pltpu.SMEM)] + [anywhere] * 5,
        out_specs=[anywhere] * 4,
        out_shape=[grad, grad, grad, jax.ShapeDtypeStruct((rows, own), f32)],
        scratch_shapes=[pltpu.VMEM(*spec) for spec in vmem] + [pltpu.SemaphoreType.DMA((s,)) for s in sems],
        compiler_params=pltpu.CompilerParams(
            collective_id=0, has_side_effects=True, vmem_limit_bytes=67043328
        ),
        name="banded_backward",
    )(lengths, queries[0], keys[0], values[0], out_grad[0], proj_weight)
    return dq[None], dk[None], dv[None], wg


def solution(mesh):
    rows = P("dp", "seq", None)
    return jax.shard_map(
        functools.partial(layer, mesh.shape["seq"], mesh.shape["dp"]),
        mesh=mesh,
        in_specs=(rows, rows, rows, rows, P("dp", None), P("dp")),
        out_specs=(rows, rows, rows, P("dp", "seq")),
        check_vma=False,
    )
```

profile of v0, /device:TPU:0, one launch (start us, length us, event | category | flops | bytes accessed | tf_op | source)
XLA Modules:
  0.0 179.8 jit_solution(4932667433773635760)
XLA Ops:
  1.3 171.5 %banded_backward.1 = (bf16[384,2048]{1,0:T(8,128)(2,1)}, bf16[384,2048]{1,0:T(8,128)(2,1)}, bf16[384,2048]{1,0:T(8,128)(2,1)}, f32[512,256]{1,0:T(8,128)}) custom-call(s32[1]{0:T(128)S(6)} %copy.14.len_ref, bf16[384,2048]{1,0:T(8,128)(2,1)} %bitcast.7, bf16[384,2048]{1,0:T(8,128)(2,1)} %bitcast.8, bf16[384,2048]{1,0:T(8,128)(2,1)} %bitcast.9, ...), custom_call_target="tpu_custom_call" | custom-call | tf_op jit(solution)/shard_map/banded_backward/pallas_call | solution.py:496
  172.7 0.0 copy-start.1
  172.8 2.8 %copy.15 = bf16[1,384,2048]{2,1,0:T(8,128)(2,1)} copy(bf16[1,384,2048]{2,1,0:T(8,128)(2,1)} %bitcast.13) | data formatting | bytes 3145728
  175.6 0.0 copy-done.1
  175.6 0.0 copy-start
  175.6 1.1 copy.16
  176.7 0.8 copy-done
  177.6 0.0 copy-start.2
  177.6 1.1 copy.17
  178.7 0.3 copy-done.2
  179.0 0.8 copy.18
Async XLA Ops:
  172.7 2.9 %copy-start.1 = (bf16[384,2048]{1,0:T(8,128)(2,1)S(1)}, bf16[384,2048]{1,0:T(8,128)(2,1)}, u32[]{:S(2)}) copy-start(bf16[384,2048]{1,0:T(8,128)(2,1)} %get-tuple-element.9) | copy-start | bytes 4718596
  175.6 2.0 %copy-start = (bf16[384,2048]{1,0:T(8,128)(2,1)S(1)}, bf16[384,2048]{1,0:T(8,128)(2,1)}, u32[]{:S(2)}) copy-start(bf16[384,2048]{1,0:T(8,128)(2,1)} %get-tuple-element.10) | copy-start | bytes 4718596
  177.6 1.4 copy-start.2
where the time goes:
time: 180 us
  Pallas kernels  171 us (95%)
  local copies, waits for them, and re-layouts  7.01 us (4%)
    pallas_call x1, Pallas kernels, layer(): pl.pallas_call(functools.partial(kernel, n, nd), in_specs=[pl.BlockSpec(m...  171 us
    unnamed x10, local copies, waits for them, and re-layouts  7.01 us

commit v1 on v0

--- a/solution.py
+++ b/solution.py
@@ -11,6 +11,7 @@
 PAIR = 2 * HEAD_DIM
 LOG2E = 1.4426950408889634
 NEG = -1e30
+LAG = 5
 MESH = pl.DeviceIdType.MESH
 
 NT = (((1,), (1,)), ((), ()))
@@ -26,8 +27,15 @@
     return i + bit - 2 * bit * lax.rem(i // bit, 2)
 
 
-def shard_order(count):
-    return [sorted(range(count), key=lambda d: (abs(d - z), d < z)) for z in range(count)]
+def pair_order(count, per):
+    orders = []
+    for z in range(count):
+        shards = sorted(range(count), key=lambda d: (abs(d - z), d < z))
+        pairs = [d * per + k for d in shards for k in range(per)]
+        if 0 < z < count - 1:
+            pairs = pairs[:1] + pairs[per:] + pairs[1:per]
+        orders.append(pairs)
+    return orders
 
 
 def pick(table, z, s):
@@ -48,10 +56,10 @@
 
 def kernel(n, nd, len_ref, q_hbm, k_hbm, v_hbm, g_hbm, w_hbm, dq_hbm, dk_hbm, dv_hbm, wg_hbm, *scratch):
     (
-        q_buf, kv, far, near, t0, t1in, behind, relay, do_buf, dq_buf, o_buf, o_in,
+        q_buf, kv, far, near, t0, t1in, behind, relay, relay2, do_buf, dq_buf, o_buf, o_in,
         g_buf, g_mine, g_send, g_in, w_buf, y_send, y_in, z_buf, z_in, kept, acc, x_send, x_in, out_buf,
         q_l, kv_l, g_l, w_l, dq_s, out_s,
-        far_s, far_r, near_s, near_r, t1_s, t1_r, ret_s, ret_r, rel_s, rel_r,
+        far_s, far_r, near_s, near_r, t1_s, t1_r, ret_s, ret_r, rel_s, rel_r, rel2_s, rel2_r,
         o_s, o_r, g_s, g_r, wu_s, wd_s, w_r, wp_s, wp_r, y_s, y_r, z_s, z_r, x_s, x_r,
     ) = scratch
     f32, bf16 = jnp.float32, jnp.bfloat16
@@ -65,15 +73,15 @@
     ahead, back = lax.rem(i + 2, n), lax.rem(i + n - 2, n)
     across = flip(i, n // 2)
     beside = flip(i, 2)
-    relayed = n == 8
+    relayed = n == 8 and steps == 8
     width = w_hbm.shape[1]
     half = width // 2
     own = width // n
     span = half // 2
-    table = shard_order(nd)
+    table = pair_order(nd, per)
 
     def pair_at(it):
-        return pick(table, z, it // per) * per + lax.rem(it, per)
+        return pick(table, z, it)
 
     def rdma(src, dst, send, recv, **where):
         return pltpu.make_async_remote_copy(
@@ -126,7 +134,8 @@
 
         every(steps, clear)
 
-    pl.semaphore_wait(barrier, len(greet))
+    with jax.named_scope("greet"):
+        pl.semaphore_wait(barrier, len(greet))
 
     def far_copy(it, a):
         return rdma(kv.at[it, a], far.at[it, a], far_s.at[2 * it + a], far_r.at[2 * it + a], seq=ahead)
@@ -146,6 +155,12 @@
     def ret_relay_out(it):
         return rdma(relay.at[it], behind.at[it, 1], rel_s.at[it], ret_r.at[2 * it + 1], seq=beside)
 
+    def ret_relay2_in(it):
+        return rdma(far.at[it, 0], relay2.at[it], ret_s.at[2 * it], rel2_r.at[it], seq=beside)
+
+    def ret_relay2_out(it):
+        return rdma(relay2.at[it], behind.at[it, 0], rel2_s.at[it], ret_r.at[2 * it], seq=across)
+
     def near_copy(src, it, a):
         return rdma(src.at[it, a], near.at[it, a], near_s.at[2 * it + a], near_r.at[2 * it + a], seq=mate)
 
@@ -168,11 +183,15 @@
         return rdma(y_send.at[it], y_in.at[it], y_s.at[it], y_r.at[it], seq=across)
 
     def z_copy(it, source, shard):
-        k = lax.rem(it, per)
+        k = lax.rem(pair_at(it), per)
         return rdma(z_buf.at[it], z_in.at[source, k], z_s.at[it], z_r.at[source * per + k], dp=shard)
 
+    def z_arrive(source, k):
+        return rdma(z_buf.at[0], z_in.at[source, k], z_s.at[0], z_r.at[source * per + k], dp=source)
+
     def first_sends(it):
-        pltpu.make_async_copy(kv.at[it], kv.at[it], kv_l.at[it]).wait()
+        with jax.named_scope("kv_load"):
+            pltpu.make_async_copy(kv.at[it], kv.at[it], kv_l.at[it]).wait()
 
         @pl.when(chip < chips - 1)
         def _():
@@ -190,13 +209,15 @@
 
     every(steps, first_sends)
 
-    for copy in own_w:
-        copy.wait()
+    with jax.named_scope("w_load"):
+        for copy in own_w:
+            copy.wait()
     for k in range(per):
         pl.when(z < nd - 1)(lambda: w_up(z * per + k).start())
         pl.when(z > 0)(lambda: w_down(z * per + k).start())
 
-    load_g.wait()
+    with jax.named_scope("g_load"):
+        load_g.wait()
     at_row = i * tokens + lax.broadcasted_iota(jnp.int32, (tokens, 1), 0)
     live = at_row < len_ref[0]
     for c in range(chips):
@@ -210,21 +231,24 @@
     g_copy.start()
 
     def halo_relay(it):
-        far_relay_in(it).wait_recv()
+        with jax.named_scope("hrel_wait"):
+            far_relay_in(it).wait_recv()
         far_relay_out(it).start()
 
     if relayed:
         pl.when(chip == chips - 1)(lambda: halo_relay(0))
 
-    g_copy.wait_recv()
+    with jax.named_scope("g_wait"):
+        g_copy.wait_recv()
     scale = HEAD_DIM ** (-0.5)
     c_exp = scale * LOG2E
 
     def begin(it):
         @pl.when(chip > 0)
         def _():
-            for a in range(2):
-                far_copy(it, a).wait_recv()
+            with jax.named_scope("far_wait"):
+                for a in range(2):
+                    far_copy(it, a).wait_recv()
 
         @pl.when(par == 1)
         def _():
@@ -232,26 +256,37 @@
                 near_copy(far, it, a).start()
 
         if relayed:
-            for extra in (1, 2):
-
-                @pl.when(jnp.logical_and(chip == chips - 1, 2 * it + extra < steps))
+            for extra in range(2):
+                at = 2 * it + extra
+
+                @pl.when(jnp.logical_and(chip == chips - 1, jnp.logical_and(at > 0, at < steps)))
                 def _():
-                    halo_relay(2 * it + extra)
+                    halo_relay(at)
 
         piece = pair_at(it)
 
-        @pl.when(it >= per)
-        def _():
-            w_mate(piece, 1 - par).wait_recv()
-
-        do = dot(g_buf[:, :half], w_buf[piece, 0], NT) + dot(g_buf[:, half:], w_buf[piece, 1], NT)
-        do_buf[...] = do.astype(bf16)
+        @pl.when(piece // per != z)
+        def _():
+            with jax.named_scope("w_wait"):
+                w_mate(piece, 1 - par).wait_recv()
+
+        with jax.named_scope("do"):
+            do = dot(g_buf[:, :half], w_buf[piece, 0], NT) + dot(g_buf[:, half:], w_buf[piece, 1], NT)
+            do_buf[...] = do.astype(bf16)
+
+    def pass_return(m):
+        @pl.when(chip == chips - 1)
+        def _():
+            with jax.named_scope("rel2_wait"):
+                ret_relay2_in(m).wait_recv()
+            ret_relay2_out(m).start()
 
     def attend(it):
         causal_keys = lax.broadcasted_iota(jnp.int32, (tokens, tokens), 0)
         causal_queries = lax.broadcasted_iota(jnp.int32, (tokens, tokens), 1)
         for a in range(2):
-            near_copy(kv, it, a).wait_recv()
+            with jax.named_scope("near_wait"):
+                near_copy(kv, it, a).wait_recv()
             q = q_buf[it, a]
             sources = (kv, near, far)
             parts, tops = [], []
@@ -296,24 +331,29 @@
                 if offset == 1:
                     t1_copy(it, a).start()
             dq_buf[it, :, a * HEAD_DIM : (a + 1) * HEAD_DIM] = (dq * scale).T.astype(bf16)
+            if a == 0:
+                pl.when(it < steps - 1)(lambda: move_weights(it))
         o_copy(it).start()
         pltpu.make_async_copy(dq_buf.at[it], dq_hbm.at[:, columns(pair_at(it) * PAIR, PAIR)], dq_s.at[it]).start()
 
     def move_weights(it):
-        j = it - 1
+        ends = jnp.logical_or(z == 0, z == nd - 1)
+        j = it - jnp.where(ends, 1, 0)
         below, above = z - 1 - j // per, z + 1 + j // per
 
-        @pl.when(jnp.logical_and(it >= 1, below >= 0))
+        @pl.when(jnp.logical_and(j >= 0, below >= 0))
         def _():
             piece = below * per + lax.rem(j, per)
-            w_up(piece).wait_recv()
+            with jax.named_scope("up_wait"):
+                w_up(piece).wait_recv()
             pl.when(z < nd - 1)(lambda: w_up(piece).start())
             w_mate(piece, par).start()
 
-        @pl.when(jnp.logical_and(it >= 1, above <= nd - 1))
+        @pl.when(jnp.logical_and(j >= 0, above <= nd - 1))
         def _():
             piece = above * per + lax.rem(j, per)
-            w_down(piece).wait_recv()
+            with jax.named_scope("down_wait"):
+                w_down(piece).wait_recv()
             pl.when(z > 0)(lambda: w_down(piece).start())
             w_mate(piece, par).start()
 
@@ -321,7 +361,8 @@
 
     def stage_a(m):
         for a in range(2):
-            t1_copy(m, a).wait_recv()
+            with jax.named_scope("t1_wait"):
+                t1_copy(m, a).wait_recv()
 
             @pl.when(par == 1)
             def _():
@@ -329,61 +370,91 @@
 
         @pl.when(chip > 0)
         def _():
-            ret_copy(m, 0).start()
             if relayed:
-                pl.when(chip != 2)(lambda: ret_copy(m, 1).start())
-                pl.when(chip == 2)(lambda: ret_relay_in(m).start())
+
+                @pl.when(chip != 2)
+                def _():
+                    ret_copy(m, 0).start()
+                    ret_copy(m, 1).start()
+
             else:
+                ret_copy(m, 0).start()
                 ret_copy(m, 1).start()
 
-        o_copy(m).wait_recv()
+        with jax.named_scope("o_wait"):
+            o_copy(m).wait_recv()
 
         def product(side):
             rows = pl.ds(pl.multiple_of(side * span, span), span)
             return dot(g_mine[rows, :], o_buf[m], NN) + dot(g_in[rows, :], o_in[m], NN)
 
-        y_send[m] = product(1 - high).astype(bf16)
-        y_copy(m).start()
-        kept[lax.rem(m, 2)] = product(high)
+        with jax.named_scope("wgrad"):
+            y_send[m] = product(1 - high).astype(bf16)
+            y_copy(m).start()
+            kept[lax.rem(m, LAG)] = product(high)
+
+    def send_around(m):
+        ret_relay2_in(m).start()
+        ret_relay_in(m).start()
+
+    def corner_return(m):
+        @pl.when(chip == 0)
+        def _():
+            with jax.named_scope("rel_wait"):
+                ret_relay_in(m).wait_recv()
+            ret_relay_out(m).start()
 
     def stage_b(m):
-        y_copy(m).wait_recv()
-        total = kept[lax.rem(m, 2)] + y_in[m].astype(f32)
-
-        @pl.when(m < per)
-        def _():
-            acc[lax.rem(m, per)] = total
-
-        @pl.when(m >= per)
+        with jax.named_scope("y_wait"):
+            y_copy(m).wait_recv()
+        total = kept[lax.rem(m, LAG)] + y_in[m].astype(f32)
+
+        pair = pair_at(m)
+
+        @pl.when(pair // per == z)
+        def _():
+            acc[lax.rem(pair, per)] = total
+
+        @pl.when(pair // per != z)
         def _():
             z_buf[m] = total.astype(bf16)
-            z_copy(m, z, pick(table, z, m // per)).start()
-
-        if relayed:
-
-            @pl.when(chip == 0)
-            def _():
-                ret_relay_in(m).wait_recv()
-                ret_relay_out(m).start()
+            z_copy(m, z, pair // per).start()
 
     def step(it):
         pl.when(it < steps)(lambda: begin(it))
         pl.when(jnp.logical_and(it >= 1, it <= steps))(lambda: stage_a(it - 1))
-        pl.when(it >= 2)(lambda: stage_b(it - 2))
+        if relayed:
+
+            @pl.when(chip == 2)
+            def _():
+                pl.when(jnp.logical_and(it >= 2, it <= 6))(lambda: send_around(it - 2))
+                pl.when(it == steps)(lambda: send_around(5))
+                pl.when(it > steps)(lambda: every(2, lambda q: send_around(6 + q)))
+
+            pl.when(it == steps)(lambda: every(2, lambda q: pass_return(q + 1)))
+        pl.when(it == LAG)(lambda: every(LAG - 2, stage_b))
+        pl.when(it >= LAG)(lambda: stage_b(it - 2))
+        if relayed:
+            pl.when(it == steps - 1)(lambda: every(3, corner_return))
+            pl.when(it >= steps)(lambda: corner_return(it - 5))
+            pl.when(it > steps)(lambda: pass_return(3))
 
         @pl.when(it < steps)
         def _():
             pltpu.make_async_copy(q_buf.at[it], q_buf.at[it], q_l.at[it]).wait()
-            attend(it)
-            pl.when(it < steps - 1)(lambda: move_weights(it))
+            with jax.named_scope("attend"):
+                attend(it)
+            if relayed:
+                pl.when(it == steps - 1)(lambda: pass_return(0))
 
     every(steps + 2, step)
 
     def finish(m):
         @pl.when(chip < chips - 1)
         def _():
-            for a in range(2):
-                ret_copy(m, a).wait_recv()
+            with jax.named_scope("ret_wait"):
+                for a in range(2):
+                    ret_copy(m, a).wait_recv()
 
         for a in range(2):
             for b, out in enumerate((dk_hbm, dv_hbm)):
@@ -394,12 +465,17 @@
                 dst = out.at[:, columns(pair_at(m) * PAIR + a * HEAD_DIM, HEAD_DIM)]
                 pltpu.make_async_copy(t0.at[m, a, b], dst, out_s.at[m]).start()
 
-    every(steps - 1, finish)
+    early = 3
+    every(early, finish)
+    if relayed:
+        every(4, lambda q: pass_return(4 + q))
+        corner_return(5)
 
     for s in range(1, nd):
         source = lax.rem(z + s, nd)
         for k in range(per):
-            z_copy(per + k, source, z).wait_recv()
+            with jax.named_scope("z_wait"):
+                z_arrive(source, k).wait_recv()
             acc[k] = acc[k] + z_in[source, k].astype(f32)
     base = jnp.int32(0)
     rows = span
@@ -421,15 +497,19 @@
             )
             sent[-1].start()
         if level == 0:
-            finish(steps - 1)
+            if relayed:
+                every(2, lambda q: corner_return(q + 6))
+            every(steps - 1 - early, lambda m: finish(m + early))
         for k in range(per):
-            sent[-per + k].wait_recv()
+            with jax.named_scope("x_wait"):
+                sent[-per + k].wait_recv()
             acc[k, stay, :] = acc[k, stay, :] + x_in[k, at, :].astype(f32)
     mine = pl.ds(pl.multiple_of(base, own), own)
     for k in range(per):
         out_buf[k * PAIR : (k + 1) * PAIR, :] = acc[k, mine, :].T
     put = pltpu.make_async_copy(out_buf, wg_hbm, g_l.at[0])
     put.start()
+    finish(steps - 1)
 
     def settle(m):
         for a in range(2):
@@ -437,14 +517,22 @@
             pl.when(chip > 0)(lambda: ret_copy(m, a).wait_send())
             t1_copy(m, a).wait_send()
         if relayed:
-            pl.when(chip == 0)(lambda: ret_relay_out(m).wait_send())
-            pl.when(chip == chips - 1)(lambda: far_relay_out(m).wait_send())
+
+            @pl.when(chip == 0)
+            def _():
+                ret_relay_out(m).wait_send()
+
+            @pl.when(chip == chips - 1)
+            def _():
+                far_relay_out(m).wait_send()
+                ret_relay2_out(m).wait_send()
+
         o_copy(m).wait_send()
         y_copy(m).wait_send()
 
-        @pl.when(m >= per)
-        def _():
-            z_copy(m, z, pick(table, z, m // per)).wait_send()
+        @pl.when(pair_at(m) // per != z)
+        def _():
+            z_copy(m, z, pair_at(m) // per).wait_send()
             w_mate(pair_at(m), par).wait_send()
 
         pl.when(jnp.logical_and(z < nd - 1, m < (z + 1) * per))(lambda: w_up(m).wait_send())
@@ -452,11 +540,30 @@
         pltpu.make_async_copy(dq_buf.at[m], dq_hbm.at[:, columns(pair_at(m) * PAIR, PAIR)], dq_s.at[m]).wait()
         pltpu.make_async_copy(t0.at[m], t0.at[m], out_s.at[m]).wait()
 
-    every(steps, settle)
+    with jax.named_scope("settle"):
+        every(steps, settle)
     g_copy.wait_send()
     for copy in sent:
         copy.wait_send()
     put.wait()
+
+
+def hand_over_kernel(*refs):
+    count = len(refs) // 2
+    for src, dst in zip(refs[:count], refs[count:]):
+        dst[...] = src[...]
+
+
+def hand_over(arrays, pieces):
+    specs = [pl.BlockSpec((a.shape[0] // pieces, a.shape[1]), lambda p: (p, 0)) for a in arrays]
+    return pl.pallas_call(
+        hand_over_kernel,
+        grid=(pieces,),
+        in_specs=specs,
+        out_specs=specs,
+        out_shape=[jax.ShapeDtypeStruct(a.shape, a.dtype) for a in arrays],
+        name="hand_over",
+    )(*arrays)
 
 
 def layer(n, nd, queries, keys, values, out_grad, proj_weight, lengths):
@@ -475,7 +582,7 @@
     vmem = [
         (head, bf16),
         *[(both, bf16)] * 6,
-        ((steps, 2, tokens, HEAD_DIM), bf16),
+        *[((steps, 2, tokens, HEAD_DIM), bf16)] * 2,
         ((tokens, PAIR), bf16),
         *[(pair, bf16)] * 3,
         ((tokens, width), bf16),
@@ -483,13 +590,13 @@
         ((steps, 2, PAIR, half), bf16),
         *[((steps, span, PAIR), bf16)] * 3,
         ((nd, per, span, PAIR), bf16),
-        ((2, span, PAIR), f32),
+        ((LAG, span, PAIR), f32),
         ((per, span, PAIR), f32),
         *[((per, span, PAIR), bf16)] * 2,
         ((rows, own), f32),
     ]
     sems = [steps, steps, 1, 2 * per, steps, steps]
-    sems += [2 * steps] * 8 + [steps] * 2
+    sems += [2 * steps] * 8 + [steps] * 4
     sems += [steps, steps, 1, 1] + [steps] * 5 + [steps] * 3 + [nd * per] + [levels * per] * 2
     anywhere = pl.BlockSpec(memory_space=pl.ANY)
     grad = jax.ShapeDtypeStruct((tokens, feat), bf16)
@@ -504,6 +611,7 @@
         ),
         name="banded_backward",
     )(lengths, queries[0], keys[0], values[0], out_grad[0], proj_weight)
+    dq, dk, dv, wg = hand_over((dq, dk, dv, wg), 4)
     return dq[None], dk[None], dv[None], wg
 
 

time: 180 us -> 137 us (0.76)
  Pallas kernels: 171 us -> 135 us
  local copies, waits for them, and re-layouts: 7.01 us -> 0 us
    pallas_call x1, Pallas kernels: 171 us -> 130 us  [layer(): pl.pallas_call(functools.partial(kernel, n, nd), in_specs=[pl.BlockSpec(m...]
    unnamed x10 -> x0, local copies, waits for them, and re-layouts: 7.01 us -> none
    pallas_call x0 -> x1, Pallas kernels: none -> 5.22 us  [hand_over(): pl.pallas_call(hand_over_kernel, grid=(pieces,), in_specs=specs, out_spec...]
where the time goes in v1:
time: 137 us
  Pallas kernels  135 us (99%)
    pallas_call x1, Pallas kernels, layer(): pl.pallas_call(functools.partial(kernel, n, nd), in_specs=[pl.BlockSpec(m...  130 us
    pallas_call x1, Pallas kernels, hand_over(): pl.pallas_call(hand_over_kernel, grid=(pieces,), in_specs=specs, out_spec...  5.22 us

profile of v1, /device:TPU:0, one launch (start us, length us, event | category | flops | bytes accessed | tf_op | source)
XLA Modules:
  0.0 136.7 jit_solution(11308234289302597860)
XLA Ops:
  1.3 130.2 %banded_backward.1 = (bf16[384,2048]{1,0:T(8,128)(2,1)}, bf16[384,2048]{1,0:T(8,128)(2,1)}, bf16[384,2048]{1,0:T(8,128)(2,1)}, f32[512,256]{1,0:T(8,128)}) custom-call(s32[1]{0:T(128)S(6)} %copy.10.len_ref, bf16[384,2048]{1,0:T(8,128)(2,1)} %bitcast.7, bf16[384,2048]{1,0:T(8,128)(2,1)} %bitcast.8, bf16[384,2048]{1,0:T(8,128)(2,1)} %bitcast.9, ...), custom_call_target="tpu_custom_call" | custom-call | tf_op jit(solution)/shard_map/banded_backward/pallas_call | solution.py:603
  131.5 5.2 %hand_over.1 = (bf16[384,2048]{1,0:T(8,128)(2,1)}, bf16[384,2048]{1,0:T(8,128)(2,1)}, bf16[384,2048]{1,0:T(8,128)(2,1)}, f32[512,256]{1,0:T(8,128)}) custom-call(bf16[384,2048]{1,0:T(8,128)(2,1)} %get-tuple-element.12.refs_0_, bf16[384,2048]{1,0:T(8,128)(2,1)} %get-tuple-element.13.refs_1_, bf16[384,2048]{1,0:T(8,128)(2,1)} %get-tuple-element.14.refs_2_, ...), custom_call_target="tpu_custom_call" | custom-call | tf_op jit(solution)/shard_map/hand_over/pallas_call | solution.py:559

commit v2 on v1

--- a/solution.py
+++ b/solution.py
@@ -11,7 +11,6 @@
 PAIR = 2 * HEAD_DIM
 LOG2E = 1.4426950408889634
 NEG = -1e30
-LAG = 5
 MESH = pl.DeviceIdType.MESH
 
 NT = (((1,), (1,)), ((), ()))
@@ -57,10 +56,10 @@
 def kernel(n, nd, len_ref, q_hbm, k_hbm, v_hbm, g_hbm, w_hbm, dq_hbm, dk_hbm, dv_hbm, wg_hbm, *scratch):
     (
         q_buf, kv, far, near, t0, t1in, behind, relay, relay2, do_buf, dq_buf, o_buf, o_in,
-        g_buf, g_mine, g_send, g_in, w_buf, y_send, y_in, z_buf, z_in, kept, acc, x_send, x_in, out_buf,
+        g_buf, g_mine, g_send, g_in, g_side, g_pass, g_far, w_buf, o_side, o_far, y_send, y_in, z_buf, z_in, acc, x_send, x_in, out_buf,
         q_l, kv_l, g_l, w_l, dq_s, out_s,
         far_s, far_r, near_s, near_r, t1_s, t1_r, ret_s, ret_r, rel_s, rel_r, rel2_s, rel2_r,
-        o_s, o_r, g_s, g_r, wu_s, wd_s, w_r, wp_s, wp_r, y_s, y_r, z_s, z_r, x_s, x_r,
+        o_s, o_r, oa_s, oa_r, of_s, of_r, g_s, g_r, wu_s, wd_s, w_r, wp_s, wp_r, y_s, y_r, z_s, z_r, x_s, x_r,
     ) = scratch
     f32, bf16 = jnp.float32, jnp.bfloat16
     i, z = lax.axis_index("seq"), lax.axis_index("dp")
@@ -73,7 +72,8 @@
     ahead, back = lax.rem(i + 2, n), lax.rem(i + n - 2, n)
     across = flip(i, n // 2)
     beside = flip(i, 2)
-    relayed = n == 8 and steps == 8
+    relayed = n == 8
+    assert steps == 8
     width = w_hbm.shape[1]
     half = width // 2
     own = width // n
@@ -103,17 +103,6 @@
         for a in range(2):
             src = q_hbm.at[:, columns(at + a * HEAD_DIM, HEAD_DIM)]
             pltpu.make_async_copy(src, q_buf.at[it, a], q_l.at[it]).start()
-
-    every(steps, load_kv)
-    load_g = pltpu.make_async_copy(g_hbm, g_buf, g_l.at[0])
-    load_g.start()
-    own_w = []
-    for k in range(per):
-        for h in range(2):
-            src = w_hbm.at[pl.ds(k * PAIR, PAIR), pl.ds(h * half, half)]
-            own_w.append(pltpu.make_async_copy(src, w_buf.at[z * per + k, h], w_l.at[2 * k + h]))
-            own_w[-1].start()
-    every(steps, load_q)
 
     bits = []
     bit = n // 2
@@ -127,6 +116,17 @@
     for who in greet:
         pl.semaphore_signal(barrier, inc=1, device_id=who, device_id_type=MESH)
 
+    every(steps, load_kv)
+    load_g = pltpu.make_async_copy(g_hbm, g_buf, g_l.at[0])
+    load_g.start()
+    own_w = []
+    for k in range(per):
+        for h in range(2):
+            src = w_hbm.at[pl.ds(k * PAIR, PAIR), pl.ds(h * half, half)]
+            own_w.append(pltpu.make_async_copy(src, w_buf.at[z * per + k, h], w_l.at[2 * k + h]))
+            own_w[-1].start()
+    every(steps, load_q)
+
     @pl.when(chip == 0)
     def _():
         def clear(it):
@@ -170,6 +170,15 @@
     def o_copy(it):
         return rdma(o_buf.at[it], o_in.at[it], o_s.at[it], o_r.at[it], seq=mate)
 
+    def o_across(it):
+        return rdma(o_buf.at[it], o_side.at[it], oa_s.at[it], oa_r.at[it], seq=across)
+
+    def o_onward(it):
+        return rdma(o_side.at[it], o_far.at[it], of_s.at[it], of_r.at[it], seq=mate)
+
+    def y_copy(it):
+        return rdma(y_send.at[it], y_in.at[it], y_s.at[it], y_r.at[it], seq=across)
+
     def w_up(piece):
         return rdma(w_buf.at[piece, par], w_buf.at[piece, par], wu_s.at[piece], w_r.at[piece], dp=lax.rem(z + 1, nd))
 
@@ -178,9 +187,6 @@
 
     def w_mate(piece, side):
         return rdma(w_buf.at[piece, side], w_buf.at[piece, side], wp_s.at[piece], wp_r.at[piece], seq=mate)
-
-    def y_copy(it):
-        return rdma(y_send.at[it], y_in.at[it], y_s.at[it], y_r.at[it], seq=across)
 
     def z_copy(it, source, shard):
         k = lax.rem(pair_at(it), per)
@@ -227,8 +233,22 @@
         g_buf[:, 2 * c * own : (2 * c + 2) * own] = jnp.concatenate([first, second], 1).astype(bf16)
         g_mine[c * own : (c + 1) * own, :] = jnp.where(par == 0, first, second).T.astype(bf16)
         g_send[c * own : (c + 1) * own, :] = jnp.where(par == 0, second, first).T.astype(bf16)
-    g_copy = rdma(g_send, g_in, g_s.at[0], g_r.at[0], seq=mate)
-    g_copy.start()
+    high = lax.rem(i // bits[0], 2)
+    held = pl.ds(pl.multiple_of(high * span, span), span)
+    given = pl.ds(pl.multiple_of((1 - high) * span, span), span)
+    g_moves = [
+        rdma(g_send, g_in, g_s.at[0], g_r.at[0], seq=mate),
+        rdma(g_mine.at[given, :], g_side, g_s.at[1], g_r.at[1], seq=across),
+        rdma(g_send.at[given, :], g_pass, g_s.at[2], g_r.at[2], seq=across),
+    ]
+    g_moves[0].start()
+
+    @pl.when(high == 1)
+    def _():
+        for copy in g_moves[1:]:
+            copy.start()
+
+    g_moves.append(rdma(g_pass, g_far, g_s.at[3], g_r.at[3], seq=mate))
 
     def halo_relay(it):
         with jax.named_scope("hrel_wait"):
@@ -238,8 +258,6 @@
     if relayed:
         pl.when(chip == chips - 1)(lambda: halo_relay(0))
 
-    with jax.named_scope("g_wait"):
-        g_copy.wait_recv()
     scale = HEAD_DIM ** (-0.5)
     c_exp = scale * LOG2E
 
@@ -273,6 +291,54 @@
         with jax.named_scope("do"):
             do = dot(g_buf[:, :half], w_buf[piece, 0], NT) + dot(g_buf[:, half:], w_buf[piece, 1], NT)
             do_buf[...] = do.astype(bf16)
+
+    def give(m):
+        with jax.named_scope("o_wait"):
+            o_copy(m).wait_recv()
+
+        @pl.when(high == 0)
+        def _():
+            with jax.named_scope("wgive"):
+                part = dot(g_mine[given, :], o_buf[m], NN) + dot(g_in[given, :], o_in[m], NN)
+                y_send[m] = part.astype(bf16)
+            y_copy(m).start()
+
+    def onward(m):
+        @pl.when(high == 0)
+        def _():
+            with jax.named_scope("oa_wait"):
+                o_across(m).wait_recv()
+            o_onward(m).start()
+
+    def combine(m):
+        @pl.when(high == 0)
+        def _():
+            with jax.named_scope("of_wait"):
+                o_onward(m).wait_recv()
+            with jax.named_scope("wgrad"):
+                total = dot(g_mine[held, :], o_buf[m], NN) + dot(g_in[held, :], o_in[m], NN)
+                total = total + dot(g_side[...], o_side[m], NN) + dot(g_far[...], o_far[m], NN)
+                place(m, total)
+
+        @pl.when(high == 1)
+        def _():
+            with jax.named_scope("y_wait"):
+                y_copy(m).wait_recv()
+            with jax.named_scope("wgrad"):
+                total = dot(g_mine[held, :], o_buf[m], NN) + dot(g_in[held, :], o_in[m], NN)
+                place(m, total + y_in[m].astype(f32))
+
+    def place(m, total):
+        pair = pair_at(m)
+
+        @pl.when(pair // per == z)
+        def _():
+            acc[lax.rem(pair, per)] = total
+
+        @pl.when(pair // per != z)
+        def _():
+            z_buf[m] = total.astype(bf16)
+            z_copy(m, z, pair // per).start()
 
     def pass_return(m):
         @pl.when(chip == chips - 1)
@@ -333,7 +399,12 @@
             dq_buf[it, :, a * HEAD_DIM : (a + 1) * HEAD_DIM] = (dq * scale).T.astype(bf16)
             if a == 0:
                 pl.when(it < steps - 1)(lambda: move_weights(it))
+
+                if relayed:
+                    pl.when(it == steps - 1)(lambda: pass_return(0))
+
         o_copy(it).start()
+        pl.when(high == 1)(lambda: o_across(it).start())
         pltpu.make_async_copy(dq_buf.at[it], dq_hbm.at[:, columns(pair_at(it) * PAIR, PAIR)], dq_s.at[it]).start()
 
     def move_weights(it):
@@ -357,7 +428,9 @@
             pl.when(z > 0)(lambda: w_down(piece).start())
             w_mate(piece, par).start()
 
-    high = lax.rem(i // bits[0], 2)
+    def send_around(m):
+        ret_relay2_in(m).start()
+        ret_relay_in(m).start()
 
     def stage_a(m):
         for a in range(2):
@@ -377,25 +450,11 @@
                     ret_copy(m, 0).start()
                     ret_copy(m, 1).start()
 
+                pl.when(jnp.logical_and(chip == 2, m < steps - 2))(lambda: send_around(m))
+
             else:
                 ret_copy(m, 0).start()
                 ret_copy(m, 1).start()
-
-        with jax.named_scope("o_wait"):
-            o_copy(m).wait_recv()
-
-        def product(side):
-            rows = pl.ds(pl.multiple_of(side * span, span), span)
-            return dot(g_mine[rows, :], o_buf[m], NN) + dot(g_in[rows, :], o_in[m], NN)
-
-        with jax.named_scope("wgrad"):
-            y_send[m] = product(1 - high).astype(bf16)
-            y_copy(m).start()
-            kept[lax.rem(m, LAG)] = product(high)
-
-    def send_around(m):
-        ret_relay2_in(m).start()
-        ret_relay_in(m).start()
 
     def corner_return(m):
         @pl.when(chip == 0)
@@ -421,33 +480,59 @@
             z_copy(m, z, pair // per).start()
 
     def step(it):
-        pl.when(it < steps)(lambda: begin(it))
-        pl.when(jnp.logical_and(it >= 1, it <= steps))(lambda: stage_a(it - 1))
+        pl.when(it == 4)(lambda: every(3, onward))
+        pl.when(it > 4)(lambda: onward(it - 2))
+        begin(it)
+
+        @pl.when(it >= 1)
+        def _():
+            stage_a(it - 1)
+            pl.when(it == 1)(g_moves[0].wait_recv)
+            give(it - 1)
+
+        @pl.when(jnp.logical_and(it == 4, high == 0))
+        def _():
+            g_moves[2].wait_recv()
+            g_moves[3].start()
+
+        @pl.when(it == 5)
+        def _():
+            @pl.when(high == 0)
+            def _():
+                g_moves[1].wait_recv()
+                g_moves[3].wait_recv()
+
+            every(3, combine)
+
+        pl.when(it > 4)(lambda: combine(it - 2))
         if relayed:
-
-            @pl.when(chip == 2)
-            def _():
-                pl.when(jnp.logical_and(it >= 2, it <= 6))(lambda: send_around(it - 2))
-                pl.when(it == steps)(lambda: send_around(5))
-                pl.when(it > steps)(lambda: every(2, lambda q: send_around(6 + q)))
-
-            pl.when(it == steps)(lambda: every(2, lambda q: pass_return(q + 1)))
-        pl.when(it == LAG)(lambda: every(LAG - 2, stage_b))
-        pl.when(it >= LAG)(lambda: stage_b(it - 2))
+            pl.when(it == steps - 1)(lambda: every(4, corner_return))
+
+        pltpu.make_async_copy(q_buf.at[it], q_buf.at[it], q_l.at[it]).wait()
+        with jax.named_scope("attend"):
+            attend(it)
         if relayed:
-            pl.when(it == steps - 1)(lambda: every(3, corner_return))
-            pl.when(it >= steps)(lambda: corner_return(it - 5))
-            pl.when(it > steps)(lambda: pass_return(3))
-
-        @pl.when(it < steps)
-        def _():
-            pltpu.make_async_copy(q_buf.at[it], q_buf.at[it], q_l.at[it]).wait()
-            with jax.named_scope("attend"):
-                attend(it)
-            if relayed:
-                pl.when(it == steps - 1)(lambda: pass_return(0))
-
-    every(steps + 2, step)
+            pl.when(it == steps - 1)(lambda: pass_return(1))
+
+    every(steps, step)
+    first_left = steps - 2
+
+    def trail(q):
+        m = first_left + q
+        onward(m)
+
+        @pl.when(q == 0)
+        def _():
+            stage_a(steps - 1)
+            give(steps - 1)
+
+        if relayed:
+            pl.when(jnp.logical_and(q == 0, chip == 2))(lambda: every(2, lambda r: send_around(steps - 2 + r)))
+            pass_return(2 + q)
+            corner_return(4 + q)
+        combine(m)
+
+    every(steps - first_left, trail)
 
     def finish(m):
         @pl.when(chip < chips - 1)
@@ -469,7 +554,7 @@
     every(early, finish)
     if relayed:
         every(4, lambda q: pass_return(4 + q))
-        corner_return(5)
+        every(2, lambda q: corner_return(6 + q))
 
     for s in range(1, nd):
         source = lax.rem(z + s, nd)
@@ -497,8 +582,6 @@
             )
             sent[-1].start()
         if level == 0:
-            if relayed:
-                every(2, lambda q: corner_return(q + 6))
             every(steps - 1 - early, lambda m: finish(m + early))
         for k in range(per):
             with jax.named_scope("x_wait"):
@@ -528,7 +611,13 @@
                 ret_relay2_out(m).wait_send()
 
         o_copy(m).wait_send()
-        y_copy(m).wait_send()
+        pl.when(high == 1)(lambda: o_across(m).wait_send())
+
+        @pl.when(high == 0)
+        def _():
+            o_onward(m).wait_send()
+            y_copy(m).wait_send()
+
 
         @pl.when(pair_at(m) // per != z)
         def _():
@@ -542,7 +631,14 @@
 
     with jax.named_scope("settle"):
         every(steps, settle)
-    g_copy.wait_send()
+    g_moves[0].wait_send()
+
+    @pl.when(high == 1)
+    def _():
+        g_moves[1].wait_send()
+        g_moves[2].wait_send()
+
+    pl.when(high == 0)(g_moves[3].wait_send)
     for copy in sent:
         copy.wait_send()
     put.wait()
@@ -587,17 +683,18 @@
         *[(pair, bf16)] * 3,
         ((tokens, width), bf16),
         *[((half, tokens), bf16)] * 3,
+        *[((span, tokens), bf16)] * 3,
         ((steps, 2, PAIR, half), bf16),
+        *[(pair, bf16)] * 2,
         *[((steps, span, PAIR), bf16)] * 3,
         ((nd, per, span, PAIR), bf16),
-        ((LAG, span, PAIR), f32),
         ((per, span, PAIR), f32),
         *[((per, span, PAIR), bf16)] * 2,
         ((rows, own), f32),
     ]
     sems = [steps, steps, 1, 2 * per, steps, steps]
     sems += [2 * steps] * 8 + [steps] * 4
-    sems += [steps, steps, 1, 1] + [steps] * 5 + [steps] * 3 + [nd * per] + [levels * per] * 2
+    sems += [steps] * 6 + [4, 4] + [steps] * 5 + [steps] * 3 + [nd * per] + [levels * per] * 2
     anywhere = pl.BlockSpec(memory_space=pl.ANY)
     grad = jax.ShapeDtypeStruct((tokens, feat), bf16)
     dq, dk, dv, wg = pl.pallas_call(
@@ -611,7 +708,7 @@
         ),
         name="banded_backward",
     )(lengths, queries[0], keys[0], values[0], out_grad[0], proj_weight)
-    dq, dk, dv, wg = hand_over((dq, dk, dv, wg), 4)
+    dq, dk, dv, wg = hand_over((dq, dk, dv, wg), 2)
     return dq[None], dk[None], dv[None], wg
 
 

time: 137 us -> 132 us (0.964)
  Pallas kernels: 135 us -> 130 us
    pallas_call x1, Pallas kernels: 130 us -> 126 us  [layer(): pl.pallas_call(functools.partial(kernel, n, nd), in_specs=[pl.BlockSpec(m...]
where the time goes in v2:
time: 132 us
  Pallas kernels  130 us (98%)
    pallas_call x1, Pallas kernels, layer(): pl.pallas_call(functools.partial(kernel, n, nd), in_specs=[pl.BlockSpec(m...  126 us
    pallas_call x1, Pallas kernels, hand_over(): pl.pallas_call(hand_over_kernel, grid=(pieces,), in_specs=specs, out_spec...  4.17 us

profile of v2, /device:TPU:0, one launch (start us, length us, event | category | flops | bytes accessed | tf_op | source)
XLA Modules:
  0.0 131.5 jit_solution(7997566848212169791)
XLA Ops:
  1.3 126.1 %banded_backward.1 = (bf16[384,2048]{1,0:T(8,128)(2,1)}, bf16[384,2048]{1,0:T(8,128)(2,1)}, bf16[384,2048]{1,0:T(8,128)(2,1)}, f32[512,256]{1,0:T(8,128)}) custom-call(s32[1]{0:T(128)S(6)} %copy.10.len_ref, bf16[384,2048]{1,0:T(8,128)(2,1)} %bitcast.7, bf16[384,2048]{1,0:T(8,128)(2,1)} %bitcast.8, bf16[384,2048]{1,0:T(8,128)(2,1)} %bitcast.9, ...), custom_call_target="tpu_custom_call" | custom-call | tf_op jit(solution)/shard_map/banded_backward/pallas_call | solution.py:700
  127.4 4.2 %hand_over.1 = (bf16[384,2048]{1,0:T(8,128)(2,1)}, bf16[384,2048]{1,0:T(8,128)(2,1)}, bf16[384,2048]{1,0:T(8,128)(2,1)}, f32[512,256]{1,0:T(8,128)}) custom-call(bf16[384,2048]{1,0:T(8,128)(2,1)} %get-tuple-element.12.refs_0_, bf16[384,2048]{1,0:T(8,128)(2,1)} %get-tuple-element.13.refs_1_, bf16[384,2048]{1,0:T(8,128)(2,1)} %get-tuple-element.14.refs_2_, ...), custom_call_target="tpu_custom_call" | custom-call | tf_op jit(solution)/shard_map/hand_over/pallas_call | solution.py:655

commit v3 on v2

--- a/solution.py
+++ b/solution.py
@@ -160,6 +160,12 @@
 
     def ret_relay2_out(it):
         return rdma(relay2.at[it], behind.at[it, 0], rel2_s.at[it], ret_r.at[2 * it], seq=across)
+
+    def shift_in(it):
+        return rdma(far.at[it, 0], relay2.at[it], ret_s.at[2 * it], rel2_r.at[it], seq=across)
+
+    def shift_out(it):
+        return rdma(relay2.at[it], behind.at[it, 0], rel2_s.at[it], ret_r.at[2 * it], seq=beside)
 
     def near_copy(src, it, a):
         return rdma(src.at[it, a], near.at[it, a], near_s.at[2 * it + a], near_r.at[2 * it + a], seq=mate)
@@ -429,8 +435,9 @@
             w_mate(piece, par).start()
 
     def send_around(m):
-        ret_relay2_in(m).start()
+        pl.when(m < steps - 1)(lambda: ret_relay2_in(m).start())
         ret_relay_in(m).start()
+        pl.when(m == steps - 1)(lambda: shift_in(m).start())
 
     def stage_a(m):
         for a in range(2):
@@ -463,21 +470,10 @@
                 ret_relay_in(m).wait_recv()
             ret_relay_out(m).start()
 
-    def stage_b(m):
-        with jax.named_scope("y_wait"):
-            y_copy(m).wait_recv()
-        total = kept[lax.rem(m, LAG)] + y_in[m].astype(f32)
-
-        pair = pair_at(m)
-
-        @pl.when(pair // per == z)
-        def _():
-            acc[lax.rem(pair, per)] = total
-
-        @pl.when(pair // per != z)
-        def _():
-            z_buf[m] = total.astype(bf16)
-            z_copy(m, z, pair // per).start()
+            @pl.when(jnp.int32(m) == steps - 1)
+            def _():
+                shift_in(m).wait_recv()
+                shift_out(m).start()
 
     def step(it):
         pl.when(it == 4)(lambda: every(3, onward))
@@ -506,7 +502,8 @@
 
         pl.when(it > 4)(lambda: combine(it - 2))
         if relayed:
-            pl.when(it == steps - 1)(lambda: every(4, corner_return))
+            pl.when(it == steps - 2)(lambda: every(4, corner_return))
+            pl.when(it == steps - 1)(lambda: corner_return(4))
 
         pltpu.make_async_copy(q_buf.at[it], q_buf.at[it], q_l.at[it]).wait()
         with jax.named_scope("attend"):
@@ -529,7 +526,7 @@
         if relayed:
             pl.when(jnp.logical_and(q == 0, chip == 2))(lambda: every(2, lambda r: send_around(steps - 2 + r)))
             pass_return(2 + q)
-            corner_return(4 + q)
+            pl.when(q == 0)(lambda: corner_return(5))
         combine(m)
 
     every(steps - first_left, trail)
@@ -553,40 +550,50 @@
     early = 3
     every(early, finish)
     if relayed:
-        every(4, lambda q: pass_return(4 + q))
+        every(3, lambda q: pass_return(4 + q))
         every(2, lambda q: corner_return(6 + q))
 
-    for s in range(1, nd):
-        source = lax.rem(z + s, nd)
-        for k in range(per):
-            with jax.named_scope("z_wait"):
-                z_arrive(source, k).wait_recv()
-            acc[k] = acc[k] + z_in[source, k].astype(f32)
     base = jnp.int32(0)
     rows = span
-    sent = []
-    for level, b in enumerate(bits[1:]):
+    levels = []
+    for b in bits[1:]:
         rows //= 2
         up = lax.rem(i // b, 2)
         away = pl.ds(pl.multiple_of(base + (1 - up) * rows, rows), rows)
         base = base + up * rows
-        stay = pl.ds(pl.multiple_of(base, rows), rows)
-        at = pl.ds(span - 2 * rows, rows)
+        levels.append((b, away, pl.ds(pl.multiple_of(base, rows), rows), pl.ds(span - 2 * rows, rows)))
+
+    def x_copy(level, k):
+        b, _, _, at = levels[level]
+        sems = (x_s.at[level * per + k], x_r.at[level * per + k])
+        return rdma(x_send.at[k, at, :], x_in.at[k, at, :], *sems, seq=flip(i, b))
+
+    def x_start(level, k):
+        _, away, _, at = levels[level]
+        x_send[k, at, :] = acc[k, away, :].astype(bf16)
+        x_copy(level, k).start()
+
+    def x_finish(level, k):
+        _, _, stay, at = levels[level]
+        with jax.named_scope("x_wait"):
+            x_copy(level, k).wait_recv()
+        acc[k, stay, :] = acc[k, stay, :] + x_in[k, at, :].astype(f32)
+
+    for k in range(per):
+        for s in range(1, nd):
+            source = lax.rem(z + s, nd)
+            with jax.named_scope("z_wait"):
+                z_arrive(source, k).wait_recv()
+            acc[k] = acc[k] + z_in[source, k].astype(f32)
+        if levels:
+            x_start(0, k)
+    every(steps - 1 - early, lambda m: finish(m + early))
+    for level in range(len(levels)):
         for k in range(per):
-            x_send[k, at, :] = acc[k, away, :].astype(bf16)
-            sent.append(
-                rdma(
-                    x_send.at[k, at, :], x_in.at[k, at, :],
-                    x_s.at[level * per + k], x_r.at[level * per + k], seq=flip(i, b),
-                )
-            )
-            sent[-1].start()
-        if level == 0:
-            every(steps - 1 - early, lambda m: finish(m + early))
+            if level:
+                x_start(level, k)
         for k in range(per):
-            with jax.named_scope("x_wait"):
-                sent[-per + k].wait_recv()
-            acc[k, stay, :] = acc[k, stay, :] + x_in[k, at, :].astype(f32)
+            x_finish(level, k)
     mine = pl.ds(pl.multiple_of(base, own), own)
     for k in range(per):
         out_buf[k * PAIR : (k + 1) * PAIR, :] = acc[k, mine, :].T
@@ -604,11 +611,12 @@
             @pl.when(chip == 0)
             def _():
                 ret_relay_out(m).wait_send()
+                pl.when(m == steps - 1)(lambda: shift_out(m).wait_send())
 
             @pl.when(chip == chips - 1)
             def _():
                 far_relay_out(m).wait_send()
-                ret_relay2_out(m).wait_send()
+                pl.when(m < steps - 1)(lambda: ret_relay2_out(m).wait_send())
 
         o_copy(m).wait_send()
         pl.when(high == 1)(lambda: o_across(m).wait_send())
@@ -639,8 +647,9 @@
         g_moves[2].wait_send()
 
     pl.when(high == 0)(g_moves[3].wait_send)
-    for copy in sent:
-        copy.wait_send()
+    for level in range(len(levels)):
+        for k in range(per):
+            x_copy(level, k).wait_send()
     put.wait()
 
 

time: 132 us -> 131 us (level); the launches traced: 132 us -> 129 us
  Pallas kernels: 130 us -> 127 us
    pallas_call x1, Pallas kernels: 126 us -> 123 us  [layer(): pl.pallas_call(functools.partial(kernel, n, nd), in_specs=[pl.BlockSpec(m...]
where the time goes in v3:
time: 131 us; the launch traced here: 129 us
  Pallas kernels  127 us (97%)
    pallas_call x1, Pallas kernels, layer(): pl.pallas_call(functools.partial(kernel, n, nd), in_specs=[pl.BlockSpec(m...  123 us
    pallas_call x1, Pallas kernels, hand_over(): pl.pallas_call(hand_over_kernel, grid=(pieces,), in_specs=specs, out_spec...  4.17 us

profile of v3, /device:TPU:0, one launch (start us, length us, event | category | flops | bytes accessed | tf_op | source)
XLA Modules:
  0.0 128.7 jit_solution(10688542951376113038)
XLA Ops:
  1.3 123.3 %banded_backward.1 = (bf16[384,2048]{1,0:T(8,128)(2,1)}, bf16[384,2048]{1,0:T(8,128)(2,1)}, bf16[384,2048]{1,0:T(8,128)(2,1)}, f32[512,256]{1,0:T(8,128)}) custom-call(s32[1]{0:T(128)S(6)} %copy.10.len_ref, bf16[384,2048]{1,0:T(8,128)(2,1)} %bitcast.7, bf16[384,2048]{1,0:T(8,128)(2,1)} %bitcast.8, bf16[384,2048]{1,0:T(8,128)(2,1)} %bitcast.9, ...), custom_call_target="tpu_custom_call" | custom-call | tf_op jit(solution)/shard_map/banded_backward/pallas_call | solution.py:709
  124.5 4.2 %hand_over.1 = (bf16[384,2048]{1,0:T(8,128)(2,1)}, bf16[384,2048]{1,0:T(8,128)(2,1)}, bf16[384,2048]{1,0:T(8,128)(2,1)}, f32[512,256]{1,0:T(8,128)}) custom-call(bf16[384,2048]{1,0:T(8,128)(2,1)} %get-tuple-element.12.refs_0_, bf16[384,2048]{1,0:T(8,128)(2,1)} %get-tuple-element.13.refs_1_, bf16[384,2048]{1,0:T(8,128)(2,1)} %get-tuple-element.14.refs_2_, ...), custom_call_target="tpu_custom_call" | custom-call | tf_op jit(solution)/shard_map/hand_over/pallas_call | solution.py:664

commit v4 on v3

--- a/solution.py
+++ b/solution.py
@@ -138,31 +138,31 @@
         pl.semaphore_wait(barrier, len(greet))
 
     def far_copy(it, a):
-        return rdma(kv.at[it, a], far.at[it, a], far_s.at[2 * it + a], far_r.at[2 * it + a], seq=ahead)
+        return rdma(kv.at[it, a], far.at[it, a], far_s.at[0], far_r.at[2 * it + a], seq=ahead)
 
     def far_relay_in(it):
-        return rdma(kv.at[it, 1], relay.at[it], far_s.at[2 * it + 1], rel_r.at[it], seq=across)
+        return rdma(kv.at[it, 1], relay.at[it], far_s.at[0], rel_r.at[it], seq=across)
 
     def far_relay_out(it):
-        return rdma(relay.at[it], far.at[it, 1], rel_s.at[it], far_r.at[2 * it + 1], seq=beside)
+        return rdma(relay.at[it], far.at[it, 1], rel_s.at[0], far_r.at[2 * it + 1], seq=beside)
 
     def ret_copy(it, a):
-        return rdma(far.at[it, a], behind.at[it, a], ret_s.at[2 * it + a], ret_r.at[2 * it + a], seq=back)
+        return rdma(far.at[it, a], behind.at[it, a], ret_s.at[0], ret_r.at[2 * it + a], seq=back)
 
     def ret_relay_in(it):
-        return rdma(far.at[it, 1], relay.at[it], ret_s.at[2 * it + 1], rel_r.at[it], seq=across)
+        return rdma(far.at[it, 1], relay.at[it], ret_s.at[0], rel_r.at[it], seq=across)
 
     def ret_relay_out(it):
-        return rdma(relay.at[it], behind.at[it, 1], rel_s.at[it], ret_r.at[2 * it + 1], seq=beside)
+        return rdma(relay.at[it], behind.at[it, 1], rel_s.at[0], ret_r.at[2 * it + 1], seq=beside)
 
     def ret_relay2_in(it):
-        return rdma(far.at[it, 0], relay2.at[it], ret_s.at[2 * it], rel2_r.at[it], seq=beside)
+        return rdma(far.at[it, 0], relay2.at[it], ret_s.at[0], rel2_r.at[it], seq=beside)
 
     def ret_relay2_out(it):
         return rdma(relay2.at[it], behind.at[it, 0], rel2_s.at[it], ret_r.at[2 * it], seq=across)
 
     def shift_in(it):
-        return rdma(far.at[it, 0], relay2.at[it], ret_s.at[2 * it], rel2_r.at[it], seq=across)
+        return rdma(far.at[it, 0], relay2.at[it], ret_s.at[0], rel2_r.at[it], seq=across)
 
     def shift_out(it):
         return rdma(relay2.at[it], behind.at[it, 0], rel2_s.at[it], ret_r.at[2 * it], seq=beside)
@@ -171,19 +171,19 @@
         return rdma(src.at[it, a], near.at[it, a], near_s.at[2 * it + a], near_r.at[2 * it + a], seq=mate)
 
     def t1_copy(it, a):
-        return rdma(near.at[it, a], t1in.at[it, a], t1_s.at[2 * it + a], t1_r.at[2 * it + a], seq=mate)
+        return rdma(near.at[it, a], t1in.at[it, a], t1_s.at[0], t1_r.at[2 * it + a], seq=mate)
 
     def o_copy(it):
-        return rdma(o_buf.at[it], o_in.at[it], o_s.at[it], o_r.at[it], seq=mate)
+        return rdma(o_buf.at[it], o_in.at[it], o_s.at[0], o_r.at[it], seq=mate)
 
     def o_across(it):
-        return rdma(o_buf.at[it], o_side.at[it], oa_s.at[it], oa_r.at[it], seq=across)
+        return rdma(o_buf.at[it], o_side.at[it], oa_s.at[0], oa_r.at[it], seq=across)
 
     def o_onward(it):
-        return rdma(o_side.at[it], o_far.at[it], of_s.at[it], of_r.at[it], seq=mate)
+        return rdma(o_side.at[it], o_far.at[it], of_s.at[0], of_r.at[it], seq=mate)
 
     def y_copy(it):
-        return rdma(y_send.at[it], y_in.at[it], y_s.at[it], y_r.at[it], seq=across)
+        return rdma(y_send.at[it], y_in.at[it], y_s.at[0], y_r.at[it], seq=across)
 
     def w_up(piece):
         return rdma(w_buf.at[piece, par], w_buf.at[piece, par], wu_s.at[piece], w_r.at[piece], dp=lax.rem(z + 1, nd))
@@ -411,7 +411,7 @@
 
         o_copy(it).start()
         pl.when(high == 1)(lambda: o_across(it).start())
-        pltpu.make_async_copy(dq_buf.at[it], dq_hbm.at[:, columns(pair_at(it) * PAIR, PAIR)], dq_s.at[it]).start()
+        pltpu.make_async_copy(dq_buf.at[it], dq_hbm.at[:, columns(pair_at(it) * PAIR, PAIR)], dq_s.at[0]).start()
 
     def move_weights(it):
         ends = jnp.logical_or(z == 0, z == nd - 1)
@@ -545,7 +545,7 @@
                 total = total + jnp.where(chip < chips - 1, behind[m, a, b].astype(f32), 0.0)
                 t0[m, a, b] = total.astype(bf16)
                 dst = out.at[:, columns(pair_at(m) * PAIR + a * HEAD_DIM, HEAD_DIM)]
-                pltpu.make_async_copy(t0.at[m, a, b], dst, out_s.at[m]).start()
+                pltpu.make_async_copy(t0.at[m, a, b], dst, out_s.at[0]).start()
 
     early = 3
     every(early, finish)
@@ -578,6 +578,16 @@
         with jax.named_scope("x_wait"):
             x_copy(level, k).wait_recv()
         acc[k, stay, :] = acc[k, stay, :] + x_in[k, at, :].astype(f32)
+
+    mine = pl.ds(pl.multiple_of(base, own), own)
+
+    def put_copy(k):
+        rows = pl.ds(k * PAIR, PAIR)
+        return pltpu.make_async_copy(out_buf.at[rows, :], wg_hbm.at[rows, :], w_l.at[k])
+
+    def deliver(k):
+        out_buf[k * PAIR : (k + 1) * PAIR, :] = acc[k, mine, :].T
+        put_copy(k).start()
 
     for k in range(per):
         for s in range(1, nd):
@@ -594,38 +604,31 @@
                 x_start(level, k)
         for k in range(per):
             x_finish(level, k)
-    mine = pl.ds(pl.multiple_of(base, own), own)
-    for k in range(per):
-        out_buf[k * PAIR : (k + 1) * PAIR, :] = acc[k, mine, :].T
-    put = pltpu.make_async_copy(out_buf, wg_hbm, g_l.at[0])
-    put.start()
+            if level == len(levels) - 1:
+                deliver(k)
     finish(steps - 1)
 
+    def sent(ref, sem):
+        pltpu.make_async_copy(ref, ref, sem.at[0]).wait()
+
+    pl.when(chip < chips - 1)(lambda: sent(kv, far_s))
+    pl.when(chip > 0)(lambda: sent(far, ret_s))
+    if relayed:
+        pl.when(jnp.logical_or(chip == 0, chip == chips - 1))(lambda: sent(relay, rel_s))
+    pl.when(high == 1)(lambda: sent(o_buf, oa_s))
+
+    @pl.when(high == 0)
+    def _():
+        sent(o_side, of_s)
+        sent(y_send, y_s)
+
+    for ref, sem in ((near, t1_s), (o_buf, o_s), (dq_buf, dq_s), (t0, out_s)):
+        sent(ref, sem)
+
     def settle(m):
-        for a in range(2):
-            pl.when(chip < chips - 1)(lambda: far_copy(m, a).wait_send())
-            pl.when(chip > 0)(lambda: ret_copy(m, a).wait_send())
-            t1_copy(m, a).wait_send()
         if relayed:
-
-            @pl.when(chip == 0)
-            def _():
-                ret_relay_out(m).wait_send()
-                pl.when(m == steps - 1)(lambda: shift_out(m).wait_send())
-
-            @pl.when(chip == chips - 1)
-            def _():
-                far_relay_out(m).wait_send()
-                pl.when(m < steps - 1)(lambda: ret_relay2_out(m).wait_send())
-
-        o_copy(m).wait_send()
-        pl.when(high == 1)(lambda: o_across(m).wait_send())
-
-        @pl.when(high == 0)
-        def _():
-            o_onward(m).wait_send()
-            y_copy(m).wait_send()
-
+            pl.when(jnp.logical_and(chip == 0, m == steps - 1))(lambda: shift_out(m).wait_send())
+            pl.when(jnp.logical_and(chip == chips - 1, m < steps - 1))(lambda: ret_relay2_out(m).wait_send())
 
         @pl.when(pair_at(m) // per != z)
         def _():
@@ -634,12 +637,11 @@
 
         pl.when(jnp.logical_and(z < nd - 1, m < (z + 1) * per))(lambda: w_up(m).wait_send())
         pl.when(jnp.logical_and(z > 0, m >= z * per))(lambda: w_down(m).wait_send())
-        pltpu.make_async_copy(dq_buf.at[m], dq_hbm.at[:, columns(pair_at(m) * PAIR, PAIR)], dq_s.at[m]).wait()
-        pltpu.make_async_copy(t0.at[m], t0.at[m], out_s.at[m]).wait()
 
     with jax.named_scope("settle"):
         every(steps, settle)
-    g_moves[0].wait_send()
+    with jax.named_scope("rest"):
+        g_moves[0].wait_send()
 
     @pl.when(high == 1)
     def _():
@@ -650,7 +652,9 @@
     for level in range(len(levels)):
         for k in range(per):
             x_copy(level, k).wait_send()
-    put.wait()
+    with jax.named_scope("put_wait"):
+        for k in range(per):
+            put_copy(k).wait()
 
 
 def hand_over_kernel(*refs):
@@ -701,9 +705,9 @@
         *[((per, span, PAIR), bf16)] * 2,
         ((rows, own), f32),
     ]
-    sems = [steps, steps, 1, 2 * per, steps, steps]
-    sems += [2 * steps] * 8 + [steps] * 4
-    sems += [steps] * 6 + [4, 4] + [steps] * 5 + [steps] * 3 + [nd * per] + [levels * per] * 2
+    sems = [steps, steps, 1, 2 * per, 1, 1]
+    sems += [1, 2 * steps, 2 * steps, 2 * steps, 1, 2 * steps, 1, 2 * steps, 1] + [steps] * 3
+    sems += [1, steps] * 3 + [4, 4] + [steps] * 5 + [1, steps, steps] + [nd * per] + [levels * per] * 2
     anywhere = pl.BlockSpec(memory_space=pl.ANY)
     grad = jax.ShapeDtypeStruct((tokens, feat), bf16)
     dq, dk, dv, wg = pl.pallas_call(

time: 131 us -> 130 us (level)
  no operation moved by 1% of the time
where the time goes in v4:
time: 130 us; the launch traced here: 128 us
  Pallas kernels  127 us (98%)
    pallas_call x1, Pallas kernels, layer(): pl.pallas_call(functools.partial(kernel, n, nd), in_specs=[pl.BlockSpec(m...  122 us
    pallas_call x1, Pallas kernels, hand_over(): pl.pallas_call(hand_over_kernel, grid=(pieces,), in_specs=specs, out_spec...  4.17 us

profile of v4, /device:TPU:0, one launch (start us, length us, event | category | flops | bytes accessed | tf_op | source)
XLA Modules:
  0.0 127.9 jit_solution(174456447949118610)
XLA Ops:
  1.3 122.4 %banded_backward.1 = (bf16[384,2048]{1,0:T(8,128)(2,1)}, bf16[384,2048]{1,0:T(8,128)(2,1)}, bf16[384,2048]{1,0:T(8,128)(2,1)}, f32[512,256]{1,0:T(8,128)}) custom-call(s32[1]{0:T(128)S(6)} %copy.10.len_ref, bf16[384,2048]{1,0:T(8,128)(2,1)} %bitcast.7, bf16[384,2048]{1,0:T(8,128)(2,1)} %bitcast.8, bf16[384,2048]{1,0:T(8,128)(2,1)} %bitcast.9, ...), custom_call_target="tpu_custom_call" | custom-call | tf_op jit(solution)/shard_map/banded_backward/pallas_call | solution.py:713
  123.7 4.2 %hand_over.1 = (bf16[384,2048]{1,0:T(8,128)(2,1)}, bf16[384,2048]{1,0:T(8,128)(2,1)}, bf16[384,2048]{1,0:T(8,128)(2,1)}, f32[512,256]{1,0:T(8,128)}) custom-call(bf16[384,2048]{1,0:T(8,128)(2,1)} %get-tuple-element.12.refs_0_, bf16[384,2048]{1,0:T(8,128)(2,1)} %get-tuple-element.13.refs_1_, bf16[384,2048]{1,0:T(8,128)(2,1)} %get-tuple-element.14.refs_2_, ...), custom_call_target="tpu_custom_call" | custom-call | tf_op jit(solution)/shard_map/hand_over/pallas_call | solution.py:668
